TPU v7x, 256 devices: a whole 4x4x8 slice. The times are simulated.
256 devices in a mesh: gx: 32 (over x_hi, z, core), gy: 8 (over y, x_lo).
Axes of the slice: x: 4 (x_hi: 2, x_lo: 2; x = x_hi * 2 + x_lo), y: 4, z: 8, core: 2. Of those that a mesh axis runs over, the one named last changes fastest.
Arguments:
- densities: float32 [192, 64, 16, 152], P('gx', 'gy'), may hold values from -6 to 6
- occupancy: int32 [192, 64, 16], P('gx', 'gy'), may hold values from 0 to 4095, as said below
- coarse_local: float32 [96, 32, 8, 152], P('gx', 'gy'), may hold values from -6 to 6
- upward_maps: float32 [8, 152, 152], replicated, may hold values from -0.15625 to 0.15625
- transfer_maps: float32 [16, 152, 152], replicated, may hold values from -0.25 to 0.25
- downward_maps: float32 [8, 152, 152], replicated, may hold values from -0.5 to 0.5
- fine_pairs: int32 [32, 8, 16, 2, 256], P('gx', 'gy'), may hold values from 0 to 2687, as said below
- parent_pairs: int32 [32, 8, 16, 2, 128], P('gx', 'gy'), may hold values from 0 to 719, as said below
Outputs:
- fine_local: float32 [192, 64, 16, 152], P('gx', 'gy')
Inputs may be any that keep to these rules, and one draw needn't show every extreme that they name: `occupancy`: A count of 0 marks an empty box. `fine_pairs`: for each device and class, 256 slots: row 0 holds a target among the device's own boxes, row 1 a source in its fine frame, at a translation of that class from the target within the target parent's neighbours' children; both boxes are occupied. Unused slots hold target 6 * 8 * 16 and source 0 and come after the used ones; on some device every slot is used. `parent_pairs`: likewise at the parent level with 128 slots; a parent is occupied where one of its children is. Unused slots hold target (3) * 4 * (8) and source 0 and come after the used ones; on some device every slot is used.
All inputs are finite; a program needn't handle non-finite values.
Results may differ from a plain program's by a relative error of at most 0.0003.
Values sent between devices are 32-bit elements; how exact they have to be, the bound alone decides.
A program may use at most 64 MiB of HBM per device.

v0:
```python
import jax
import jax.numpy as jnp
from jax import lax
from jax.sharding import PartitionSpec as P

RIM = 3


highest = lax.Precision.HIGHEST
level_scale = 0.5


def extended(cells, sides, width):
    for axis, dim in sides:
        count = lax.axis_size(axis)
        ends = count - 1
        head = lax.slice_in_dim(cells, 0, width, axis=dim)
        tail = lax.slice_in_dim(cells, cells.shape[dim] - width, cells.shape[dim], axis=dim)
        cells = jnp.concatenate(
            [
                lax.ppermute(tail, axis, [(i, (i + 1) % count) for i in range(ends)]),
                cells,
                lax.ppermute(head, axis, [((i + 1) % count, i) for i in range(ends)]),
            ],
            axis=dim,
        )
    return cells


def lift_children(children, upward_maps):
    extent_x, extent_y, extent_z, columns = children.shape
    grouped = children.reshape(extent_x // 2, 2, extent_y // 2, 2, extent_z // 2, 2, columns)
    matrices = upward_maps.reshape(2, 2, 2, columns, columns)
    return jnp.einsum("aibjckp,ijkpq->abcq", grouped, matrices, precision=highest)


def push_down(parents, downward_maps):
    extent_x, extent_y, extent_z, columns = parents.shape
    matrices = downward_maps.reshape(2, 2, 2, columns, columns)
    spread = jnp.einsum("abcp,ijkpq->aibjckq", parents, matrices, precision=highest)
    return spread.reshape(2 * extent_x, 2 * extent_y, 2 * extent_z, columns)


def apply_pairs(framed, pairs, transfer_maps, boxes):
    columns = framed.shape[-1]
    flat_frame = framed.reshape(-1, columns)
    gathered = flat_frame[pairs[:, 1, :]]
    carried = jnp.einsum("csp,cpq->csq", gathered, transfer_maps, precision=highest)
    targets = pairs[:, 0, :].reshape(-1)
    return (
        jnp.zeros((boxes, columns), jnp.float32)
        .at[targets]
        .add(carried.reshape(-1, columns), mode="drop")
    )


def per_device(
    densities,
    occupancy,
    coarse_local,
    upward_maps,
    transfer_maps,
    downward_maps,
    fine_pairs,
    parent_pairs,
):
    filled = occupancy > 0
    masked = jnp.where(filled[..., None], densities, jnp.zeros_like(densities))
    width_x, width_y, layers, columns = masked.shape
    fine_frame = extended(masked, (("gx", 0), ("gy", 1)), RIM)
    parent_frame = extended(lift_children(masked, upward_maps), (("gx", 0), ("gy", 1)), RIM)
    fine_check = apply_pairs(
        fine_frame, fine_pairs[0, 0], transfer_maps, width_x * width_y * layers
    )
    parent_shape = coarse_local.shape
    parent_boxes = parent_shape[0] * parent_shape[1] * parent_shape[2]
    parent_local = coarse_local.reshape(-1, columns) + level_scale * apply_pairs(
        parent_frame, parent_pairs[0, 0], transfer_maps, parent_boxes
    )
    fine_local = fine_check.reshape(masked.shape) + push_down(
        parent_local.reshape(parent_shape), downward_maps
    )
    return jnp.where(filled[..., None], fine_local, jnp.zeros_like(fine_local))


def solution(mesh):
    return jax.shard_map(
        per_device,
        mesh=mesh,
        in_specs=(
            P("gx", "gy", None, None),
            P("gx", "gy", None),
            P("gx", "gy", None, None),
            P(),
            P(),
            P(),
            P("gx", "gy", None, None, None),
            P("gx", "gy", None, None, None),
        ),
        out_specs=P("gx", "gy", None, None),
        check_vma=False,
    )
```

profile of v0, /device:TPU:1, one launch (start us, length us, event | category | flops | bytes accessed | tf_op | source)
XLA Modules:
  0.0 152.6 jit_solution(3030770736549301860)
XLA Ops:
  0.0 0.0 copy-start
  0.0 0.9 broadcast_compare_fusion
  0.9 1.3 broadcast_select_fusion
  2.2 0.0 copy-start.1
  2.2 0.0 copy-start.6
  2.2 0.0 copy-start.7
  2.2 1.4 reshape.150
  3.6 2.6 %convolution_bitcast_fusion.1 = f32[3,4,8,152]{3,2,1,0:T(8,128)S(1)} fusion(f32[2,2,2,152,152,1,1]{4,3,2,1,0,6,5:T(8,128)} %bitcast.65, f32[3,2,4,2,8,2,152]{6,5,4,3,2,1,0:T(2,128)} %reshape.150), kind=kOutput, calls=%fused_computation.6 | convolution fusion | flops 212926464 | bytes 1264640 | tf_op jit(solution)/shard_map/aibjckp,ijkpq->abcq/dot_general | solution.py:34
  6.2 4.9 %collective-permute-start.4 = (f32[3,4,8,152]{3,2,1,0:T(8,128)S(1)}, f32[3,4,8,152]{3,2,1,0:T(8,128)S(1)}, u32[]{:S(2)}, u32[]{:S(2)}) collective-permute-start(f32[3,4,8,152]{3,2,1,0:T(8,128)S(1)} %convolution_bitcast_fusion.1), channel_id=1, source_target_pairs={{0,8},{8,16},{16,24},{24,32},{32,40},{40,48},{48,56},{56,64},{64,7... | collective-permute-start | bytes 175112 | tf_op jit(solution)/shard_map/ppermute | solution.py:21
  11.1 1.9 %collective-permute-start.5 = (f32[3,4,8,152]{3,2,1,0:T(8,128)S(1)}, f32[3,4,8,152]{3,2,1,0:T(8,128)S(1)}, u32[]{:S(2)}, u32[]{:S(2)}) collective-permute-start(f32[3,4,8,152]{3,2,1,0:T(8,128)S(1)} %convolution_bitcast_fusion.1), channel_id=1, source_target_pairs={{8,0},{16,8},{24,16},{32,24},{40,32},{48,40},{56,48},{64,56},{72,6... | collective-permute-start | bytes 175112 | tf_op jit(solution)/shard_map/ppermute | solution.py:23
  13.1 0.9 fusion.7
  14.0 0.0 copy-done.1
  14.0 3.6 %collective-permute-start = (f32[3,8,16,152]{3,2,1,0:T(8,128)}, f32[3,8,16,152]{3,2,1,0:T(8,128)}, u32[]{:S(2)}, u32[]{:S(2)}) collective-permute-start(f32[3,8,16,152]{3,2,1,0:T(8,128)} %get-tuple-element.7), channel_id=1, source_target_pairs={{0,8},{8,16},{16,24},{24,32},{32,40},{40,48},{48,56},{56,64},{64,7... | collective-permute-start | bytes 700424 | tf_op jit(solution)/shard_map/ppermute | solution.py:21
  17.7 1.9 %collective-permute-start.1 = (f32[3,8,16,152]{3,2,1,0:T(8,128)}, f32[3,8,16,152]{3,2,1,0:T(8,128)}, u32[]{:S(2)}, u32[]{:S(2)}) collective-permute-start(f32[3,8,16,152]{3,2,1,0:T(8,128)} %get-tuple-element.8), channel_id=1, source_target_pairs={{8,0},{16,8},{24,16},{32,24},{40,32},{48,40},{56,48},{64,56},{72,6... | collective-permute-start | bytes 700424 | tf_op jit(solution)/shard_map/ppermute | solution.py:23
  19.6 0.0 copy-done.6
  19.6 0.0 copy-done.7
  19.7 0.0 collective-permute-done.4
  19.7 0.0 collective-permute-done.5
  19.8 3.1 %collective-permute-start.6 = (f32[9,3,8,152]{3,2,1,0:T(8,128)S(1)}, f32[9,3,8,152]{3,2,1,0:T(8,128)S(1)}, u32[]{:S(2)}, u32[]{:S(2)}) collective-permute-start(f32[9,3,8,152]{3,2,1,0:T(8,128)S(1)} %get-tuple-element.9), channel_id=1, source_target_pairs={{0,1},{1,2},{2,3},{3,4},{4,5},{5,6},{6,7},{8,9},{9,10},{10,11},{11... | collective-permute-start | bytes 393992 | tf_op jit(solution)/shard_map/ppermute | solution.py:21
  23.0 1.3 collective-permute-start.7
  24.3 7.5 %collective-permute-done.6 = f32[9,3,8,152]{3,2,1,0:T(8,128)S(1)} collective-permute-done((f32[9,3,8,152]{3,2,1,0:T(8,128)S(1)}, f32[9,3,8,152]{3,2,1,0:T(8,128)S(1)}, u32[]{:S(2)}, u32[]{:S(2)}) %collective-permute-start.6) | collective-permute-done | bytes 131360 | tf_op jit(solution)/shard_map/ppermute | solution.py:21
  31.8 6.4 %collective-permute-done.7 = f32[9,3,8,152]{3,2,1,0:T(8,128)S(1)} collective-permute-done((f32[9,3,8,152]{3,2,1,0:T(8,128)S(1)}, f32[9,3,8,152]{3,2,1,0:T(8,128)S(1)}, u32[]{:S(2)}, u32[]{:S(2)}) %collective-permute-start.7) | collective-permute-done | bytes 131360 | tf_op jit(solution)/shard_map/ppermute | solution.py:23
  38.2 0.1 pad_maximum_fusion.1
  38.3 8.6 %gather_fusion.1 = f32[2048,152]{1,0:T(8,128)} fusion(f32[720,152]{1,0:T(8,128)S(1)} %bitcast.59, s32[2048]{0:T(1024)S(1)} %fusion.6), kind=kCustom, calls=%fused_computation.1 | custom fusion | bytes 2498560 | tf_op jit(solution)/shard_map/gather | solution.py:47
  46.8 0.0 copy-done
  46.9 0.0 copy-start.2
  46.9 5.1 %fusion.10 = f32[16,128,152]{2,1,0:T(8,128)} fusion(f32[16,128,152]{2,1,0:T(8,128)} %bitcast.61, f32[16,152,152]{2,1,0:T(8,128)S(1)} %copy-done), kind=kOutput, calls=%fused_computation.33 | convolution fusion | flops 567803904 | bytes 3969024 | tf_op jit(solution)/shard_map/reshape | solution.py:53
  52.0 0.0 copy-start.5
  52.0 12.0 %scatter_custom_fusion.1 = f32[96,152]{1,0:T(8,128)S(1)} fusion(s32[2048]{0:T(1024)S(1)} %bitcast.76, f32[2048,152]{1,0:T(8,128)} %bitcast.64, f32[]{:T(128)} %constant.8.clone.1), kind=kCustom, calls=%fused_computation.20 | custom fusion | flops 311296 | bytes 58880 | tf_op jit(solution)/shard_map/scatter-add | solution.py:53
  64.0 0.0 copy-start.4
  64.0 0.0 collective-permute-done
  64.0 0.0 collective-permute-done.1
  64.0 0.0 copy-done.2
  64.0 2.4 %pad_maximum_fusion.4 = (f32[12,3,16,152]{3,2,1,0:T(8,128)}, f32[12,3,16,152]{3,2,1,0:T(8,128)}) fusion(f32[3,8,16,152]{3,2,1,0:T(8,128)} %collective-permute-done.1, f32[6,8,16,152]{3,2,1,0:T(8,128)S(1)} %copy-done.2, f32[3,8,16,152]{3,2,1,0:T(8,128)} %collective-permute-done), kind=kLoop, calls=%fused_computation.12 | loop fusion | flops 350208 | bytes 1634304 | tf_op jit(solution)/shard_map/slice | solution.py:18
  66.4 3.9 %collective-permute-start.2 = (f32[12,3,16,152]{3,2,1,0:T(8,128)}, f32[12,3,16,152]{3,2,1,0:T(8,128)}, u32[]{:S(2)}, u32[]{:S(2)}) collective-permute-start(f32[12,3,16,152]{3,2,1,0:T(8,128)} %get-tuple-element.5), channel_id=1, source_target_pairs={{0,1},{1,2},{2,3},{3,4},{4,5},{5,6},{6,7},{8,9},{9,10},{10,11},{11... | collective-permute-start | bytes 1050632 | tf_op jit(solution)/shard_map/ppermute | solution.py:21
  70.4 1.5 collective-permute-start.3
  71.8 0.0 copy-done.5
  71.9 0.0 copy-done.4
  71.9 0.9 convolution_bitcast_fusion
  72.7 1.3 copy.31
  74.0 2.6 %reshape.156 = f32[6,8,16,152]{3,2,1,0:T(8,128)} reshape(f32[3,2,4,2,8,2,152]{6,5,4,3,2,1,0:T(2,128)} %copy.31) | data formatting | bytes 933888 | tf_op jit(solution)/shard_map/reshape | solution.py:41
  76.7 5.8 %collective-permute-done.2 = f32[12,3,16,152]{3,2,1,0:T(8,128)} collective-permute-done((f32[12,3,16,152]{3,2,1,0:T(8,128)}, f32[12,3,16,152]{3,2,1,0:T(8,128)}, u32[]{:S(2)}, u32[]{:S(2)}) %collective-permute-start.2) | collective-permute-done | bytes 350240 | tf_op jit(solution)/shard_map/ppermute | solution.py:21
  82.5 14.6 %collective-permute-done.3 = f32[12,3,16,152]{3,2,1,0:T(8,128)} collective-permute-done((f32[12,3,16,152]{3,2,1,0:T(8,128)}, f32[12,3,16,152]{3,2,1,0:T(8,128)}, u32[]{:S(2)}, u32[]{:S(2)}) %collective-permute-start.3) | collective-permute-done | bytes 350240 | tf_op jit(solution)/shard_map/ppermute | solution.py:23
  97.1 3.5 %pad_maximum_fusion = f32[12,14,16,152]{3,2,1,0:T(8,128)} fusion(f32[12,3,16,152]{3,2,1,0:T(8,128)} %collective-permute-done.3, f32[3,8,16,152]{3,2,1,0:T(8,128)} %collective-permute-done.1, f32[6,8,16,152]{3,2,1,0:T(8,128)S(1)} %copy-done.2, f32[3,8,16,152]{3,2,1,0:T(8,128)} %collective-permute-done, f32[12,3,16,152]{3,2,1,0:T(8,128)} %collective-permute-done.2), kind=kLoop, calls=%fused_computation.4 | loop fusion | flops 1634304 | bytes 3268608 | tf_op jit(solution)/shard_map/concatenate | solution.py:19
  100.6 17.8 %gather_fusion = f32[4096,152]{1,0:T(8,128)} fusion(f32[2688,152]{1,0:T(8,128)} %bitcast.58, s32[4096]{0:T(1024)S(1)} %broadcast_clamp_fusion), kind=kCustom, calls=%fused_computation | custom fusion | bytes 4997120 | tf_op jit(solution)/shard_map/gather | solution.py:47
  118.5 0.0 copy-start.3
  118.5 8.2 %fusion.9 = f32[16,256,152]{2,1,0:T(8,128)} fusion(f32[16,256,152]{2,1,0:T(8,128)} %bitcast.60, f32[16,152,152]{2,1,0:T(8,128)S(1)} %copy-done), kind=kOutput, calls=%fused_computation.32 | convolution fusion | flops 1135607808 | bytes 6459392 | tf_op jit(solution)/shard_map/reshape | solution.py:53
  126.7 23.7 %scatter_custom_fusion = f32[768,152]{1,0:T(8,128)} fusion(s32[4096]{0:T(1024)S(1)} %bitcast.75, f32[4096,152]{1,0:T(8,128)} %bitcast.62, f32[]{:T(128)} %constant.8.clone.1), kind=kCustom, calls=%fused_computation.14 | custom fusion | flops 622592 | bytes 467456 | tf_op jit(solution)/shard_map/scatter-add | solution.py:53
  150.4 0.0 copy-done.3
  150.4 2.2 %add_select_fusion = f32[6,8,16,152]{3,2,1,0:T(8,128)} fusion(f32[6,8,16,152]{3,2,1,0:T(8,128)} %bitcast.63, f32[6,8,16,152]{3,2,1,0:T(8,128)S(1)} %copy-done.3, pred[6,8,16]{2,1,0:T(8,128)(4,1)S(1)} %broadcast_compare_fusion), kind=kLoop, calls=%fused_computation.8 | loop fusion | flops 233472 | bytes 1401600 | tf_op jit(solution)/shard_map/jit(_where)/select_n | solution.py:83
  (10 shorter events, 0.2 us)
Async XLA Ops:
  0.0 46.8 %copy-start = (f32[16,152,152]{2,1,0:T(8,128)S(1)}, f32[16,152,152]{2,1,0:T(8,128)}, u32[]{:S(2)}) copy-start(f32[16,152,152]{2,1,0:T(8,128)} %param.12) | copy-start | bytes 4435972
  2.2 11.8 %copy-start.1 = (f32[6,8,16,152]{3,2,1,0:T(8,128)}, f32[6,8,16,152]{3,2,1,0:T(8,128)S(1)}, u32[]{:S(2)}) copy-start(f32[6,8,16,152]{3,2,1,0:T(8,128)S(1)} %broadcast_select_fusion) | copy-start | bytes 1400836
  2.2 17.4 %copy-start.6 = (s32[1,1,16,2,256]{4,3,2,1,0:T(2,128)S(1)}, s32[1,1,16,2,256]{4,3,2,1,0:T(2,128)}, u32[]{:S(2)}) copy-start(s32[1,1,16,2,256]{4,3,2,1,0:T(2,128)} %param.14) | copy-start | bytes 98308
  2.2 17.4 %copy-start.7 = (s32[1,1,16,2,128]{4,3,2,1,0:T(2,128)S(1)}, s32[1,1,16,2,128]{4,3,2,1,0:T(2,128)}, u32[]{:S(2)}) copy-start(s32[1,1,16,2,128]{4,3,2,1,0:T(2,128)} %param.15) | copy-start | bytes 49156
  6.2 13.5 %collective-permute-start.4 = (f32[3,4,8,152]{3,2,1,0:T(8,128)S(1)}, f32[3,4,8,152]{3,2,1,0:T(8,128)S(1)}, u32[]{:S(2)}, u32[]{:S(2)}) collective-permute-start(f32[3,4,8,152]{3,2,1,0:T(8,128)S(1)} %convolution_bitcast_fusion.1), channel_id=1, source_target_pairs={{0,8},{8,16},{16,24},{24,32},{32,40},{40,48},{48,56},{56,64},{64,7... | collective-permute-start | bytes 175112 | tf_op jit(solution)/shard_map/ppermute | solution.py:21
  11.1 8.6 %collective-permute-start.5 = (f32[3,4,8,152]{3,2,1,0:T(8,128)S(1)}, f32[3,4,8,152]{3,2,1,0:T(8,128)S(1)}, u32[]{:S(2)}, u32[]{:S(2)}) collective-permute-start(f32[3,4,8,152]{3,2,1,0:T(8,128)S(1)} %convolution_bitcast_fusion.1), channel_id=1, source_target_pairs={{8,0},{16,8},{24,16},{32,24},{40,32},{48,40},{56,48},{64,56},{72,6... | collective-permute-start | bytes 175112 | tf_op jit(solution)/shard_map/ppermute | solution.py:23
  14.0 50.0 %collective-permute-start = (f32[3,8,16,152]{3,2,1,0:T(8,128)}, f32[3,8,16,152]{3,2,1,0:T(8,128)}, u32[]{:S(2)}, u32[]{:S(2)}) collective-permute-start(f32[3,8,16,152]{3,2,1,0:T(8,128)} %get-tuple-element.7), channel_id=1, source_target_pairs={{0,8},{8,16},{16,24},{24,32},{32,40},{40,48},{48,56},{56,64},{64,7... | collective-permute-start | bytes 700424 | tf_op jit(solution)/shard_map/ppermute | solution.py:21
  17.7 46.4 %collective-permute-start.1 = (f32[3,8,16,152]{3,2,1,0:T(8,128)}, f32[3,8,16,152]{3,2,1,0:T(8,128)}, u32[]{:S(2)}, u32[]{:S(2)}) collective-permute-start(f32[3,8,16,152]{3,2,1,0:T(8,128)} %get-tuple-element.8), channel_id=1, source_target_pairs={{8,0},{16,8},{24,16},{32,24},{40,32},{48,40},{56,48},{64,56},{72,6... | collective-permute-start | bytes 700424 | tf_op jit(solution)/shard_map/ppermute | solution.py:23
  19.8 11.9 %collective-permute-start.6 = (f32[9,3,8,152]{3,2,1,0:T(8,128)S(1)}, f32[9,3,8,152]{3,2,1,0:T(8,128)S(1)}, u32[]{:S(2)}, u32[]{:S(2)}) collective-permute-start(f32[9,3,8,152]{3,2,1,0:T(8,128)S(1)} %get-tuple-element.9), channel_id=1, source_target_pairs={{0,1},{1,2},{2,3},{3,4},{4,5},{5,6},{6,7},{8,9},{9,10},{10,11},{11... | collective-permute-start | bytes 393992 | tf_op jit(solution)/shard_map/ppermute | solution.py:21
  23.0 15.2 %collective-permute-start.7 = (f32[9,3,8,152]{3,2,1,0:T(8,128)S(1)}, f32[9,3,8,152]{3,2,1,0:T(8,128)S(1)}, u32[]{:S(2)}, u32[]{:S(2)}) collective-permute-start(f32[9,3,8,152]{3,2,1,0:T(8,128)S(1)} %get-tuple-element.10), channel_id=1, source_target_pairs={{1,0},{2,1},{3,2},{4,3},{5,4},{6,5},{7,6},{9,8},{10,9},{11,10},{12... | collective-permute-start | bytes 393992 | tf_op jit(solution)/shard_map/ppermute | solution.py:23
  46.9 17.2 %copy-start.2 = (f32[6,8,16,152]{3,2,1,0:T(8,128)S(1)}, f32[6,8,16,152]{3,2,1,0:T(8,128)}, u32[]{:S(2)}) copy-start(f32[6,8,16,152]{3,2,1,0:T(8,128)} %copy-done.1) | copy-start | bytes 1400836
  52.0 19.9 %copy-start.5 = (f32[3,4,8,152]{3,2,1,0:T(8,128)S(1)}, f32[3,4,8,152]{3,2,1,0:T(8,128)}, u32[]{:S(2)}) copy-start(f32[3,4,8,152]{3,2,1,0:T(8,128)} %param.10) | copy-start | bytes 175108
  64.0 7.9 %copy-start.4 = (f32[8,152,152]{2,1,0:T(8,128)S(1)}, f32[8,152,152]{2,1,0:T(8,128)}, u32[]{:S(2)}) copy-start(f32[8,152,152]{2,1,0:T(8,128)} %param.13) | copy-start | bytes 2217988
  66.4 16.1 %collective-permute-start.2 = (f32[12,3,16,152]{3,2,1,0:T(8,128)}, f32[12,3,16,152]{3,2,1,0:T(8,128)}, u32[]{:S(2)}, u32[]{:S(2)}) collective-permute-start(f32[12,3,16,152]{3,2,1,0:T(8,128)} %get-tuple-element.5), channel_id=1, source_target_pairs={{0,1},{1,2},{2,3},{3,4},{4,5},{5,6},{6,7},{8,9},{9,10},{10,11},{11... | collective-permute-start | bytes 1050632 | tf_op jit(solution)/shard_map/ppermute | solution.py:21
  70.4 26.8 %collective-permute-start.3 = (f32[12,3,16,152]{3,2,1,0:T(8,128)}, f32[12,3,16,152]{3,2,1,0:T(8,128)}, u32[]{:S(2)}, u32[]{:S(2)}) collective-permute-start(f32[12,3,16,152]{3,2,1,0:T(8,128)} %get-tuple-element.6), channel_id=1, source_target_pairs={{1,0},{2,1},{3,2},{4,3},{5,4},{6,5},{7,6},{9,8},{10,9},{11,10},{12... | collective-permute-start | bytes 1050632 | tf_op jit(solution)/shard_map/ppermute | solution.py:23
  118.5 32.0 %copy-start.3 = (f32[6,8,16,152]{3,2,1,0:T(8,128)S(1)}, f32[6,8,16,152]{3,2,1,0:T(8,128)}, u32[]{:S(2)}) copy-start(f32[6,8,16,152]{3,2,1,0:T(8,128)} %reshape.156) | copy-start | bytes 1400836
where the time goes:
time: 153 us
  other arithmetic  46.2 us (30%)
  waiting for transfers between devices  34.4 us (22%)
  local copies, waits for them, and re-layouts  32.7 us (21%)
  starting transfers between devices  22.2 us (15%)
  matrix products  16.8 us (11%)
    scatter-add x2, other arithmetic, apply_pairs(): return jnp.zeros((boxes, columns), jnp.float32).at[targets].add(carried.r...  35.8 us
    gather x2, local copies, waits for them, and re-layouts, apply_pairs(): gathered = flat_frame[pairs[:, 1, :]]  26.4 us
    ppermute x4, waiting for transfers between devices, extended(): lax.ppermute(head, axis, [((i + 1) % count, i) for i in range(ends)])  21.1 us
    ppermute x4, starting transfers between devices, extended(): lax.ppermute(tail, axis, [(i, (i + 1) % count) for i in range(ends)])  15.6 us
    reshape x2, matrix products, apply_pairs(): carried.reshape(-1, columns)  13.3 us
    ppermute x4, waiting for transfers between devices, extended(): lax.ppermute(tail, axis, [(i, (i + 1) % count) for i in range(ends)])  13.3 us
    ppermute x4, starting transfers between devices, extended(): lax.ppermute(head, axis, [((i + 1) % count, i) for i in range(ends)])  6.59 us
    concatenate x3, other arithmetic, extended(): jnp.concatenate([lax.ppermute(tail, axis, [(i, (i + 1) % count) for i in...  3.59 us
  transfers between devices with their start and end apart: 8, of which 4 were waited for; matrix products, arithmetic and copies ran while one was open for 21% of the time, Pallas kernels for 0%

commit v1 on v0

v1 whole, which is shorter than its diff:
```python
import jax
import jax.numpy as jnp
from jax import lax
from jax.experimental import pallas as pl
from jax.experimental.pallas import tpu as pltpu
from jax.sharding import PartitionSpec as P

f32, bf16, i32 = jnp.float32, jnp.bfloat16, jnp.int32
COEF = 152
CLASSES = 16
CAPF = 256
CAPP = 128
LEVEL_SCALE = 0.5
MESH = pl.DeviceIdType.MESH

TILES = 22


def dot(a, b):
    return lax.dot_general(a, b, (((1,), (0,)), ((), ())), preferred_element_type=f32)


def split(x):
    hi = x.astype(bf16)
    return hi, (x - hi.astype(f32)).astype(bf16)


def stacked(x):
    x = jnp.concatenate([x, jnp.zeros((8, x.shape[1]), f32)], axis=0)
    hi, lo = split(x)
    return jnp.concatenate([hi, lo], axis=0)


def fine_position(s):
    u = s >> 4
    fx = (u * 147) >> 11
    x = fx - 3
    y = u - fx * 14 - 3
    z = s & 15
    below, above = y < 0, y >= 8
    inner = jnp.where(
        below,
        768 + x * 32 + (y + 2) * 16,
        jnp.where(above, 1024 + x * 32 + (y - 8) * 16, x * 128 + y * 16),
    )
    xs = jnp.where(x < 0, x + 2, x - 6)
    base = jnp.where(x < 0, 1280, 1664)
    outer = base + jnp.where(
        below,
        256 + xs * 32 + (y + 2) * 16,
        jnp.where(above, 320 + xs * 32 + (y - 8) * 16, xs * 128 + y * 16),
    )
    return jnp.where((x >= 0) & (x < 6), inner, outer) + z


def parent_position(s):
    u = s >> 3
    fx = (u * 103) >> 10
    x = fx - 3
    y = u - fx * 10 - 3
    z = s & 7
    below, above = y < 0, y >= 4
    base = jnp.where(x < 0, 256, jnp.where(x >= 3, 512, 0))
    xs = jnp.where(x < 0, x + 3, jnp.where(x >= 3, x - 3, x))
    return (
        base
        + jnp.where(
            below,
            128 + xs * 16 + (y + 2) * 8,
            jnp.where(above, 192 + xs * 16 + (y - 4) * 8, xs * 32 + y * 8),
        )
        + z
    )


def kernel(
    shape,
    dens_hbm, occ_ref, coarse_ref, up_hbm, maps_hbm, down_hbm, fp_ref, pp_ref,
    out_ref,
    dens, up, maps, down, occ_pad, rows, frame, frame2, corner, tpad, tmaps, dmaps,
    tgt_pad, tgt_f, tgt_p, pos_f, pos_p, carried_f, carried_p, psum,
    load_sem, send_sem, recv_sem,
):
    mesh_x, mesh_y = shape
    a = lax.axis_index("gx")
    b = lax.axis_index("gy")
    has_l, has_r = a > 0, a < mesh_x - 1
    has_d, has_u = b > 0, b < mesh_y - 1
    left, right = (a - 1, b), (a + 1, b)
    down_n, up_n = (a, b - 1), (a, b + 1)

    loads = [
        pltpu.make_async_copy(src, dst, load_sem.at[n])
        for n, (src, dst) in enumerate(
            [(dens_hbm, dens), (up_hbm, up), (maps_hbm, maps), (down_hbm, down)]
        )
    ]
    for copy in loads:
        copy.start()

    barrier = pltpu.get_barrier_semaphore()
    neighbours = ((has_l, left), (has_r, right), (has_d, down_n), (has_u, up_n))
    for there, who in neighbours:

        @pl.when(there)
        def _():
            pl.semaphore_signal(barrier, inc=1, device_id=who, device_id_type=MESH)

    occ_pad[...] = jnp.zeros_like(occ_pad)
    occ_pad[0:48, 0:16] = (occ_ref[...] > 0).astype(f32)
    mask_t = occ_pad[...].T[0:16, :]
    loads[0].wait()
    rows[1] = jnp.zeros((768, 128), f32)
    for n in range(48):
        keep = mask_t[:, n : n + 1] > 0
        here = dens[n * 16 : n * 16 + 16, :]
        here = jnp.where(keep, here, jnp.zeros_like(here))
        rows[0, n * 16 : n * 16 + 16, :] = here[:, 0:128]
        rows[1, n * 16 : n * 16 + 16, 0 : COEF - 128] = here[:, 128:COEF]

    pl.semaphore_wait(
        barrier, sum(there.astype(i32) for there, _ in neighbours)
    )

    def boxes(at):
        return jnp.concatenate([rows[0, at, :], rows[1, at, :]], axis=1)

    def face(y0, x0, x1):
        return [boxes(pl.ds(x * 128 + y0 * 16, 32)) for x in range(x0, x1)]

    def send(n, src, dst, who):
        return pltpu.make_async_remote_copy(
            src_ref=src, dst_ref=dst, send_sem=send_sem.at[n], recv_sem=recv_sem.at[n],
            device_id=who, device_id_type=MESH,
        )

    ycopies = [
        (send(0, corner.at[0], frame.at[8], down_n), has_d, has_u),
        (send(1, corner.at[2], frame.at[6], up_n), has_u, has_d),
        (send(2, corner.at[1], frame.at[9], down_n), has_d, has_u),
        (send(3, corner.at[3], frame.at[7], up_n), has_u, has_d),
    ]
    xcopies = [
        (send(4, frame.at[pl.ds(0, 2)], frame.at[pl.ds(13, 2)], left), has_l, has_r),
        (send(5, frame.at[pl.ds(4, 2)], frame.at[pl.ds(10, 2)], right), has_r, has_l),
        (send(6, frame.at[16], frame.at[20], left), has_l, has_r),
        (send(7, frame.at[16], frame.at[18], right), has_r, has_l),
    ]
    ccopies = [
        (send(8, corner.at[4], frame.at[15], left), has_l, has_r),
        (send(9, corner.at[5], frame.at[12], right), has_r, has_l),
        (send(10, frame.at[17], frame.at[21], left), has_l, has_r),
        (send(11, frame.at[17], frame.at[19], right), has_r, has_l),
    ]

    def start(copies):
        for copy, sends, _ in copies:

            @pl.when(sends)
            def _():
                copy.start()

    def arrive(copies):
        for copy, _, gets in copies:

            @pl.when(gets)
            def _():
                copy.wait_recv()

    for missing, tiles in (
        (jnp.logical_not(has_d), (6, 7)),
        (jnp.logical_not(has_u), (8, 9)),
        (jnp.logical_not(has_l), (10, 11, 12, 18, 19)),
        (jnp.logical_not(has_r), (13, 14, 15, 20, 21)),
    ):

        @pl.when(missing)
        def _():
            for t in tiles:
                frame[t] = jnp.zeros((COEF, 128), f32)

    def turned(pieces):
        return jnp.concatenate(pieces, axis=0).T[0:COEF, :]

    corner[0] = turned(face(0, 0, 4))
    corner[2] = turned(face(6, 0, 4))
    start(ycopies[0:2])

    loads[1].wait()
    parents = jnp.zeros((96, COEF), f32)
    for k in range(8):
        ci, cj, ck = k >> 2, (k >> 1) & 1, k & 1
        child = jnp.concatenate(
            [
                boxes(pl.ds((2 * px + ci) * 128 + (2 * py + cj) * 16 + ck, 8, stride=2))
                for px in range(3)
                for py in range(4)
            ],
            axis=0,
        )[:, 0:COEF]
        chi, clo = split(child)
        uhi, ulo = split(up[k])
        parents = parents + (dot(chi, uhi) + (dot(clo, uhi) + dot(chi, ulo)))
    pad = jnp.zeros((96, 256 - COEF), f32)
    parents = jnp.concatenate([parents, pad], axis=1)
    for side, y0 in ((0, 0), (1, 2)):
        pieces = face(6 * side, 4, 6)
        pieces += [parents[x * 32 + y0 * 8 : x * 32 + y0 * 8 + 16, :] for x in range(3)]
        pieces += [jnp.zeros((16, 256), f32)]
        corner[2 * side + 1] = turned(pieces)
    start(ycopies[2:4])
    for x in (0, 1, 4, 5):
        frame[x] = boxes(pl.ds(x * 128, 128)).T[0:COEF, :]
    frame[16] = turned([parents, jnp.zeros((32, 256), f32)])
    start(xcopies)
    for x in (2, 3):
        frame[x] = boxes(pl.ds(x * 128, 128)).T[0:COEF, :]

    pos_f[...] = fine_position(fp_ref[:, 1, :])
    pos_p[...] = parent_position(pp_ref[:, 1, :])
    tgt_pad[...] = jnp.zeros_like(tgt_pad)
    tgt_pad[0:16, 0:256] = fp_ref[:, 0, :].astype(f32)
    tgt_pad[0:16, 256:384] = pp_ref[:, 0, :].astype(f32)
    tgt_f[...] = tgt_pad[:, 0:256].T
    tgt_p[...] = tgt_pad[:, 256:384].T
    tpad[...] = jnp.zeros_like(tpad)
    loads[2].wait()

    def turn_map(c, carry):
        m = maps[c]
        hi = m.astype(bf16).astype(f32)
        tpad[0:152, 0:152] = hi
        tpad[160:312, 0:152] = hi
        tpad[320:472, 0:152] = m - hi
        tmaps[c] = tpad[...].T[0:160, :].astype(bf16)
        return carry

    lax.fori_loop(0, CLASSES, turn_map, 0)
    loads[3].wait()
    for k in range(8):
        dhi, dlo = split(down[k])
        dmaps[k, 0] = dhi
        dmaps[k, 1] = dlo
    for t in (0, 1, 2, 3, 4, 5, 16):
        frame2[t] = stacked(frame[t])

    arrive(ycopies)
    lane = lax.broadcasted_iota(i32, (COEF, 128), 1)
    first = lane < 64
    corner[4] = jnp.where(first, frame[6], pltpu.roll(frame[8], 64, 1))
    corner[5] = jnp.where(first, frame[7], pltpu.roll(frame[9], 64, 1))
    frame[17] = jnp.where(first, pltpu.roll(frame[7], 64, 1), frame[9])
    start(ccopies)
    for t in (6, 7, 8, 9, 17):
        frame2[t] = stacked(frame[t])
    arrive(xcopies)
    arrive(ccopies)
    for t in (10, 11, 12, 13, 14, 15, 18, 19, 20, 21):
        frame2[t] = stacked(frame[t])

    sub = lax.broadcasted_iota(i32, (256, 256), 0)

    def pick(first_tile, pairs, place):
        total = None
        for n in range(pairs):
            hot = jnp.where(sub + n * 256 == place, 1.0, 0.0).astype(bf16)
            t = first_tile + 2 * n
            part = dot(jnp.concatenate([frame2[t], frame2[t + 1]], axis=1), hot)
            total = part if total is None else total + part
        return total.astype(bf16)

    def carry_over(c, g):
        g3 = jnp.concatenate(
            [g, g[0:160, :], jnp.zeros((32, g.shape[1]), bf16)], axis=0
        )
        return stacked(dot(tmaps[c], g3)[0:COEF, :])

    def fine_class(c, carry):
        g = pick(0, 8, pos_f[pl.ds(c, 1), :])
        carried_f[c] = carry_over(c, g)
        return carry

    lax.fori_loop(0, CLASSES, fine_class, 0)

    def parent_class(h, carry):
        c = 2 * h
        place = jnp.concatenate([pos_p[pl.ds(c, 1), :], pos_p[pl.ds(c + 1, 1), :]], axis=1)
        g = pick(16, 3, place)
        carried_p[h] = jnp.concatenate(
            [carry_over(c, g[:, 0:128]), carry_over(c + 1, g[:, 128:256])], axis=1
        )
        return carry

    lax.fori_loop(0, CLASSES // 2, parent_class, 0)

    total = None
    plane = lax.broadcasted_iota(i32, (128, 128), 1).astype(f32)
    for h in range(CLASSES // 2):
        hot = jnp.concatenate(
            [
                jnp.where(plane == tgt_p[:, c : c + 1], 1.0, 0.0).astype(bf16)
                for c in (2 * h, 2 * h + 1)
            ],
            axis=0,
        )
        part = dot(carried_p[h], hot)
        total = part if total is None else total + part
    psum[...] = jnp.zeros_like(psum)
    psum[0:COEF, :] = total[0:COEF, :] + total[160:312, :]
    local = coarse_ref[...] + LEVEL_SCALE * psum[...].T[0:96, 0:COEF]
    lhi, llo = split(local)

    fplane = lax.broadcasted_iota(i32, (256, 256), 1).astype(f32)
    for n in range(3):
        total = None
        for c in range(CLASSES):
            hot = jnp.where(fplane + n * 256.0 == tgt_f[:, c : c + 1], 1.0, 0.0).astype(bf16)
            part = dot(carried_f[c], hot)
            total = part if total is None else total + part
        summed = total[0:COEF, :] + total[160:312, :]
        summed = jnp.concatenate([summed, jnp.zeros((104, 256), f32)], axis=0)
        turned_back = summed.T
        rows[0, n * 256 : n * 256 + 256, :] = turned_back[:, 0:128]
        rows[1, n * 256 : n * 256 + 256, :] = turned_back[:, 128:256]

    for k in range(8):
        ci, cj, ck = k >> 2, (k >> 1) & 1, k & 1
        pushed = dot(lhi, dmaps[k, 0]) + (dot(llo, dmaps[k, 0]) + dot(lhi, dmaps[k, 1]))
        pushed = jnp.concatenate([pushed, pad], axis=1)
        for px in range(3):
            for py in range(4):
                at = pl.ds((2 * px + ci) * 128 + (2 * py + cj) * 16 + ck, 8, stride=2)
                n = (px * 4 + py) * 8
                rows[0, at, :] = rows[0, at, :] + pushed[n : n + 8, 0:128]
                rows[1, at, :] = rows[1, at, :] + pushed[n : n + 8, 128:256]
    for n in range(48):
        keep = mask_t[:, n : n + 1] > 0
        here = boxes(pl.ds(n * 16, 16))[:, 0:COEF]
        out_ref[n * 16 : n * 16 + 16, :] = jnp.where(keep, here, jnp.zeros_like(here))

    for copies in (ycopies, xcopies, ccopies):
        for copy, sends, _ in copies:

            @pl.when(sends)
            def _():
                copy.wait_send()


def per_device(shape, dens, occ, coarse, up, maps, down, fp, pp):
    import functools

    anyspace = pl.BlockSpec(memory_space=pl.ANY)
    vmem = pl.BlockSpec(memory_space=pltpu.VMEM)
    out = pl.pallas_call(
        functools.partial(kernel, shape),
        out_shape=jax.ShapeDtypeStruct((768, COEF), f32),
        in_specs=[anyspace, vmem, vmem, anyspace, anyspace, anyspace, vmem, vmem],
        out_specs=vmem,
        scratch_shapes=[
            pltpu.VMEM((768, COEF), f32),
            pltpu.VMEM((8, COEF, COEF), f32),
            pltpu.VMEM((CLASSES, COEF, COEF), f32),
            pltpu.VMEM((8, COEF, COEF), f32),
            pltpu.VMEM((128, 128), f32),
            pltpu.VMEM((2, 768, 128), f32),
            pltpu.VMEM((TILES, COEF, 128), f32),
            pltpu.VMEM((TILES, 320, 128), bf16),
            pltpu.VMEM((6, COEF, 128), f32),
            pltpu.VMEM((512, 256), f32),
            pltpu.VMEM((CLASSES, 160, 512), bf16),
            pltpu.VMEM((8, 2, COEF, COEF), bf16),
            pltpu.VMEM((128, 384), f32),
            pltpu.VMEM((256, 128), f32),
            pltpu.VMEM((128, 128), f32),
            pltpu.VMEM((CLASSES, CAPF), i32),
            pltpu.VMEM((CLASSES, CAPP), i32),
            pltpu.VMEM((CLASSES, 320, CAPF), bf16),
            pltpu.VMEM((CLASSES // 2, 320, 256), bf16),
            pltpu.VMEM((256, 128), f32),
            pltpu.SemaphoreType.DMA((4,)),
            pltpu.SemaphoreType.DMA((12,)),
            pltpu.SemaphoreType.DMA((12,)),
        ],
        compiler_params=pltpu.CompilerParams(
            collective_id=0, has_side_effects=True, vmem_limit_bytes=56 * 1024 * 1024
        ),
    )(
        dens.reshape(768, COEF),
        occ.reshape(48, 16),
        coarse.reshape(96, COEF),
        up,
        maps,
        down,
        fp[0, 0],
        pp[0, 0],
    )
    return out.reshape(dens.shape)


def solution(mesh):
    import functools

    shape = (mesh.shape["gx"], mesh.shape["gy"])
    return jax.shard_map(
        functools.partial(per_device, shape),
        mesh=mesh,
        in_specs=(
            P("gx", "gy", None, None),
            P("gx", "gy", None),
            P("gx", "gy", None, None),
            P(),
            P(),
            P(),
            P("gx", "gy", None, None, None),
            P("gx", "gy", None, None, None),
        ),
        out_specs=P("gx", "gy", None, None),
        check_vma=False,
    )
```

time: 153 us -> 43.7 us (0.29)
  the two profiles are of different devices: /device:TPU:1 before, /device:TPU:221 now
where the time goes in v1:
time: 43.7 us; the launch traced here: 43.6 us
  Pallas kernels  41.5 us (95%)
  local copies, waits for them, and re-layouts  2.1 us (5%)
    pallas_call x1, Pallas kernels, per_device(): pl.pallas_call(functools.partial(kernel, shape), out_shape=jax.ShapeDtype...  41.5 us
    unnamed x1, local copies, waits for them, and re-layouts  2.1 us

profile of v1, /device:TPU:221, one launch (start us, length us, event | category | flops | bytes accessed | tf_op | source)
XLA Modules:
  0.0 43.6 jit_solution(13528284875571952054)
XLA Ops:
  0.0 41.5 %shard_map.82 = f32[768,152]{1,0:T(8,128)} custom-call(f32[768,152]{1,0:T(8,128)} %bitcast.7, s32[48,16]{1,0:T(8,128)} %bitcast.10, f32[96,152]{1,0:T(8,128)} %bitcast.8, f32[8,152,152]{2,1,0:T(8,128)} %up_hbm.1, f32[16,152,152]{2,1,0:T(8,128)} %maps_hbm.1, f32[8,152,152]{2,1,0:T(8,128)} %down_hbm.1, s32[16,2,256]{2,1,0:T(2,128)} %bitcast.9, ...), custom_call_target="tpu_custom_call" | custom-call | tf_op jit(solution)/shard_map/pallas_call | solution.py:354
  41.5 2.1 %copy.10 = f32[6,8,16,152]{3,2,1,0:T(8,128)} copy(f32[6,8,16,152]{3,2,1,0:T(8,128)} %bitcast.6) | data formatting | bytes 933888

commit v2 on v1

v2 whole, which is shorter than its diff:
```python
import functools

import jax
import jax.numpy as jnp
from jax import lax
from jax.experimental import pallas as pl
from jax.experimental.pallas import tpu as pltpu
from jax.sharding import PartitionSpec as P

f32, bf16, i32 = jnp.float32, jnp.bfloat16, jnp.int32
COEF = 152
CLASSES = 16
CAPF = 256
CAPP = 128
LEVEL_SCALE = 0.5
MESH = pl.DeviceIdType.MESH

TILES = 22


def dot(a, b):
    return lax.dot_general(a, b, (((1,), (0,)), ((), ())), preferred_element_type=f32)


def split(x):
    hi = x.astype(bf16)
    return hi, (x - hi.astype(f32)).astype(bf16)


def stacked(x):
    hi = x.astype(bf16).astype(f32)
    return jnp.concatenate([hi, x - hi], axis=0).astype(bf16)


def fine_position(s):
    u = s >> 4
    fx = (u * 147) >> 11
    x = fx - 3
    y = u - fx * 14 - 3
    z = s & 15
    below, above = y < 0, y >= 8
    yo = jnp.where(below, y + 2, y - 8) * 16
    middle = (x >= 2) & (x < 4)
    xa = jnp.where(x >= 4, x - 2, x)
    edge = jnp.where(middle, 1536 + (x - 2) * 32, 768 + xa * 32)
    edge = edge + jnp.where(above, 128, 0) + yo
    inner = jnp.where(below | above, edge, x * 128 + y * 16)
    right = x >= 6
    xs = jnp.where(right, x - 6, x + 2)
    side = jnp.where(right, 1280, 1024) + xs * 128 + y * 16
    corner = jnp.where(right, 1920, 1792) + jnp.where(above, 64, 0) + xs * 32 + yo
    outer = jnp.where(below | above, corner, side)
    return jnp.where((x >= 0) & (x < 6), inner, outer) + z


def parent_position(s):
    u = s >> 3
    fx = (u * 103) >> 10
    x = fx - 3
    y = u - fx * 10 - 3
    z = s & 7
    below, above = y < 0, y >= 4
    yo = jnp.where(below, y + 2, y - 4) * 8
    left, right = x < 0, x >= 3
    xs = jnp.where(left, x + 3, jnp.where(right, x - 3, x))
    straight = jnp.where(left, 256, jnp.where(right, 384, 0)) + xs * 32 + y * 8
    corner = jnp.where(left, 512, jnp.where(right, 640, 128)) + jnp.where(above, 64, 0)
    return jnp.where(below | above, corner + xs * 16 + yo, straight) + z


def kernel(
    shape,
    dens_hbm, occ_hbm, coarse_hbm, up_hbm, maps_hbm, down_hbm, fp_hbm, pp_hbm,
    sums, local, dmaps, mask_out,
    dens, up, maps, down, occ, coarse, fp, pp,
    occ_pad, rows, frame, frame2, corner, tpad, tmaps,
    tgt_pad, tgt_f, tgt_p, pos_f, pos_p, picked_f, picked_p, carried_f, carried_p, psum,
    load_sem, send_sem, recv_sem,
):
    mesh_x, mesh_y = shape
    a = lax.axis_index("gx")
    b = lax.axis_index("gy")
    has_l, has_r = a > 0, a < mesh_x - 1
    has_d, has_u = b > 0, b < mesh_y - 1
    left, right = (a - 1, b), (a + 1, b)
    down_n, up_n = (a, b - 1), (a, b + 1)

    barrier = pltpu.get_barrier_semaphore()
    neighbours = ((has_l, left), (has_r, right), (has_d, down_n), (has_u, up_n))
    loads = [
        pltpu.make_async_copy(src, dst, load_sem.at[n])
        for n, (src, dst) in enumerate(
            [
                (occ_hbm, occ), (dens_hbm, dens), (up_hbm, up), (fp_hbm, fp),
                (pp_hbm, pp), (maps_hbm, maps), (down_hbm, down), (coarse_hbm, coarse),
            ]
        )
    ]
    for copy in loads[0:3]:
        copy.start()
    for there, who in neighbours:

        @pl.when(there)
        def _():
            pl.semaphore_signal(barrier, inc=1, device_id=who, device_id_type=MESH)

    for copy in loads[3:]:
        copy.start()

    for missing, tiles in (
        (jnp.logical_not(has_d), (6, 12)),
        (jnp.logical_not(has_u), (7, 13)),
        (jnp.logical_not(has_l), (8, 9, 14, 18, 20)),
        (jnp.logical_not(has_r), (10, 11, 15, 19, 21)),
    ):

        @pl.when(missing)
        def _():
            for t in tiles:
                frame[t] = jnp.zeros((COEF, 128), f32)

    occ_pad[...] = jnp.zeros_like(occ_pad)
    rows[1] = jnp.zeros((768, 128), f32)
    tgt_pad[...] = jnp.zeros_like(tgt_pad)
    tpad[...] = jnp.zeros_like(tpad)
    psum[...] = jnp.zeros_like(psum)

    loads[0].wait()
    occ_pad[0:48, 0:16] = (occ[...] > 0).astype(f32)
    mask_t = occ_pad[...].T[0:16, :]
    mask_out[...] = mask_t
    loads[1].wait()
    for n in range(48):
        keep = mask_t[:, n : n + 1] > 0
        here = dens[n * 16 : n * 16 + 16, :]
        here = jnp.where(keep, here, jnp.zeros_like(here))
        rows[0, n * 16 : n * 16 + 16, :] = here[:, 0:128]
        rows[1, n * 16 : n * 16 + 16, 0 : COEF - 128] = here[:, 128:COEF]

    def boxes(at):
        return jnp.concatenate([rows[0, at, :], rows[1, at, :]], axis=1)

    def face(y0, xs):
        return [boxes(pl.ds(x * 128 + y0 * 16, 32)) for x in xs]

    def send(n, src, dst, who):
        return pltpu.make_async_remote_copy(
            src_ref=src, dst_ref=dst, send_sem=send_sem.at[n], recv_sem=recv_sem.at[n],
            device_id=who, device_id_type=MESH,
        )

    y_first = [
        (send(0, corner.at[0], frame.at[7], down_n), has_d, has_u),
        (send(1, corner.at[1], frame.at[6], up_n), has_u, has_d),
    ]
    y_second = [
        (send(2, corner.at[2], frame.at[13], down_n), has_d, has_u),
        (send(3, corner.at[3], frame.at[12], up_n), has_u, has_d),
    ]
    x_fine = [
        (send(4, frame.at[pl.ds(0, 2)], frame.at[pl.ds(10, 2)], left), has_l, has_r),
        (send(5, frame.at[pl.ds(4, 2)], frame.at[pl.ds(8, 2)], right), has_r, has_l),
    ]
    x_parent = [
        (send(6, frame.at[16], frame.at[19], left), has_l, has_r),
        (send(7, frame.at[16], frame.at[18], right), has_r, has_l),
    ]
    c_fine = [
        (send(8, corner.at[4], frame.at[15], left), has_l, has_r),
        (send(9, corner.at[5], frame.at[14], right), has_r, has_l),
    ]
    c_parent = [
        (send(10, frame.at[17], frame.at[21], left), has_l, has_r),
        (send(11, frame.at[17], frame.at[20], right), has_r, has_l),
    ]

    def start(copies):
        for copy, sends, _ in copies:

            @pl.when(sends)
            def _():
                copy.start()

    def arrive(copies):
        for copy, _, gets in copies:

            @pl.when(gets)
            def _():
                copy.wait_recv()

    def turned(pieces):
        return jnp.concatenate(pieces, axis=0).T[0:COEF, :]

    corner[0] = turned(face(0, (0, 1, 4, 5)))
    corner[1] = turned(face(6, (0, 1, 4, 5)))
    pl.semaphore_wait(barrier, sum(there.astype(i32) for there, _ in neighbours))
    start(y_first)
    for x in (0, 1, 4, 5):
        frame[x] = boxes(pl.ds(x * 128, 128)).T[0:COEF, :]
    start(x_fine)

    loads[2].wait()
    parents = None
    for k in range(8):
        ci, cj, ck = k >> 2, (k >> 1) & 1, k & 1
        child = jnp.concatenate(
            [
                boxes(pl.ds((2 * px + ci) * 128 + (2 * py + cj) * 16 + ck, 8, stride=2))
                for px in range(3)
                for py in range(4)
            ],
            axis=0,
        )[:, 0:COEF]
        chi, clo = split(child)
        uhi, ulo = split(up[k])
        lifted = dot(chi, uhi) + (dot(clo, uhi) + dot(chi, ulo))
        parents = lifted if parents is None else parents + lifted
    parents = jnp.concatenate([parents, jnp.zeros((96, 256 - COEF), f32)], axis=1)
    for side, y0 in ((0, 0), (1, 2)):
        pieces = face(6 * side, (2, 3))
        pieces += [parents[x * 32 + y0 * 8 : x * 32 + y0 * 8 + 16, :] for x in range(3)]
        pieces += [jnp.zeros((16, 256), f32)]
        corner[side + 2] = turned(pieces)
    start(y_second)
    frame[16] = turned([parents, jnp.zeros((32, 256), f32)])
    start(x_parent)
    for x in (2, 3):
        frame[x] = boxes(pl.ds(x * 128, 128)).T[0:COEF, :]

    def doubled(*tiles):
        for t in tiles:
            frame2[t] = stacked(frame[t])

    doubled(0, 1, 2, 3, 4, 5, 16)
    loads[3].wait()
    loads[4].wait()
    pos_f[...] = fine_position(fp[:, 1, :])
    pos_p[...] = parent_position(pp[:, 1, :])
    tgt_pad[0:16, 0:256] = fp[:, 0, :].astype(f32)
    tgt_pad[0:16, 256:384] = pp[:, 0, :].astype(f32)
    tgt_f[...] = tgt_pad[:, 0:256].T
    tgt_p[...] = tgt_pad[:, 256:384].T

    sub = lax.broadcasted_iota(i32, (256, 256), 0)

    def pick(first_tile, pairs, place):
        total = None
        for n in pairs:
            hot = jnp.where(sub == place - n * 256, 1.0, 0.0).astype(bf16)
            t = first_tile + 2 * n
            part = dot(jnp.concatenate([frame2[t], frame2[t + 1]], axis=1), hot)
            total = part if total is None else total + part
        return total.astype(bf16)

    def parent_place(h):
        return jnp.concatenate(
            [pos_p[pl.ds(2 * h, 1), :], pos_p[pl.ds(2 * h + 1, 1), :]], axis=1
        )

    def carry_over(c, g):
        n = g.shape[1]
        g3 = jnp.concatenate([g, g[0:160, :], jnp.zeros((48, n), bf16)], axis=0)
        return stacked(dot(tmaps[c], g3)[0:COEF, :])

    def own_stage(h, carry):
        for c in (2 * h, 2 * h + 1):
            picked_f[c] = pick(0, (0, 1, 2), pos_f[pl.ds(c, 1), :])
        return carry

    lax.fori_loop(0, CLASSES // 2, own_stage, 0)

    arrive(y_first)
    first = lax.broadcasted_iota(i32, (COEF, 128), 1) < 64
    corner[4] = jnp.where(first, frame[6], pltpu.roll(frame[7], 64, 1))
    corner[5] = jnp.where(first, pltpu.roll(frame[6], 64, 1), frame[7])
    start(c_fine)

    loads[5].wait()

    def turn_map(c, carry):
        m = maps[c]
        hi = m.astype(bf16).astype(f32)
        tpad[0:152, 0:152] = hi
        tpad[152:304, 0:152] = hi
        tpad[304:456, 0:152] = m - hi
        tmaps[c] = tpad[...].T[0:160, :].astype(bf16)
        return carry

    lax.fori_loop(0, CLASSES, turn_map, 0)

    arrive(y_second)
    frame[17] = jnp.where(first, pltpu.roll(frame[12], 64, 1), frame[13])
    start(c_parent)

    loads[6].wait()
    for k in range(8):
        dhi, dlo = split(down[k])
        dmaps[k, 0] = dhi
        dmaps[k, 1] = dlo
    arrive(x_fine)
    doubled(6, 7, 8, 9, 10, 11)

    def side_stage(h, carry):
        for c in (2 * h, 2 * h + 1):
            g = pick(0, (3, 4, 5), pos_f[pl.ds(c, 1), :])
            picked_f[c] = picked_f[c] + g
        return carry

    lax.fori_loop(0, CLASSES // 2, side_stage, 0)

    arrive(x_parent)
    arrive(c_fine)
    doubled(12, 13, 14, 15, 17, 18, 19)

    def last_stage(h, carry):
        for c in (2 * h, 2 * h + 1):
            g = picked_f[c] + pick(0, (6, 7), pos_f[pl.ds(c, 1), :])
            carried_f[c] = carry_over(c, g)
        picked_p[h] = pick(16, (0, 1), parent_place(h))
        return carry

    lax.fori_loop(0, CLASSES // 2, last_stage, 0)

    fplane = lax.broadcasted_iota(i32, (256, 256), 1).astype(f32)
    for n in range(3):
        total = None
        for c in range(CLASSES):
            hot = jnp.where(fplane == tgt_f[:, c : c + 1] - n * 256.0, 1.0, 0.0).astype(bf16)
            part = dot(carried_f[c], hot)
            total = part if total is None else total + part
        summed = total[0:COEF, :] + total[COEF : 2 * COEF, :]
        summed = jnp.concatenate([summed, jnp.zeros((104, 256), f32)], axis=0)
        turned_back = summed.T
        sums[0, n * 256 : n * 256 + 256, :] = turned_back[:, 0:128]
        sums[1, n * 256 : n * 256 + 256, :] = turned_back[:, 128:256]

    arrive(c_parent)
    doubled(20, 21)

    def parent_stage(h, carry):
        g = picked_p[h] + pick(16, (2,), parent_place(h))
        carried_p[h] = jnp.concatenate(
            [carry_over(2 * h, g[:, 0:128]), carry_over(2 * h + 1, g[:, 128:256])], axis=1
        )
        return carry

    lax.fori_loop(0, CLASSES // 2, parent_stage, 0, unroll=2)

    total = None
    plane = lax.broadcasted_iota(i32, (128, 128), 1).astype(f32)
    for h in range(CLASSES // 2):
        hot = jnp.concatenate(
            [
                jnp.where(plane == tgt_p[:, c : c + 1], 1.0, 0.0).astype(bf16)
                for c in (2 * h, 2 * h + 1)
            ],
            axis=0,
        )
        part = dot(carried_p[h], hot)
        total = part if total is None else total + part
    psum[0:COEF, :] = total[0:COEF, :] + total[COEF : 2 * COEF, :]
    loads[7].wait()
    expansion = coarse[...] + LEVEL_SCALE * psum[...].T[0:96, 0:COEF]
    lhi, llo = split(expansion)
    local[0] = lhi
    local[1] = llo

    for copies in (y_first, y_second, x_fine, x_parent, c_fine, c_parent):
        for copy, sends, _ in copies:

            @pl.when(sends)
            def _():
                copy.wait_send()


def finish(sums, local, dmaps, mask, out_hbm, rows, out, sem):
    pad = jnp.zeros((96, 256 - COEF), f32)
    lhi, llo = local[0], local[1]
    rows[...] = sums[...]
    pushed = []
    for k in range(8):
        p = dot(lhi, dmaps[k, 0]) + (dot(llo, dmaps[k, 0]) + dot(lhi, dmaps[k, 1]))
        pushed.append(jnp.concatenate([p, pad], axis=1))
    mask_t = mask[...]
    copies = []
    for px in range(3):
        for k in range(8):
            ci, cj, ck = k >> 2, (k >> 1) & 1, k & 1
            for py in range(4):
                at = pl.ds((2 * px + ci) * 128 + (2 * py + cj) * 16 + ck, 8, stride=2)
                n = (px * 4 + py) * 8
                rows[0, at, :] = rows[0, at, :] + pushed[k][n : n + 8, 0:128]
                rows[1, at, :] = rows[1, at, :] + pushed[k][n : n + 8, 128:256]
        for n in range(px * 16, px * 16 + 16):
            keep = mask_t[:, n : n + 1] > 0
            at = pl.ds(n * 16, 16)
            here = jnp.concatenate([rows[0, at, :], rows[1, at, :]], axis=1)[:, 0:COEF]
            out[at, :] = jnp.where(keep, here, jnp.zeros_like(here))
        part = pl.ds(px * 256, 256)
        copy = pltpu.make_async_copy(out.at[part], out_hbm.at[part], sem.at[px])
        copy.start()
        copies.append(copy)
    for copy in copies:
        copy.wait()


def per_device(shape, dens, occ, coarse, up, maps, down, fp, pp):
    vmem = pl.BlockSpec(memory_space=pltpu.VMEM)
    parts = pl.pallas_call(
        functools.partial(kernel, shape),
        out_shape=(
            jax.ShapeDtypeStruct((2, 768, 128), f32),
            jax.ShapeDtypeStruct((2, 96, COEF), bf16),
            jax.ShapeDtypeStruct((8, 2, COEF, COEF), bf16),
            jax.ShapeDtypeStruct((16, 128), f32),
        ),
        in_specs=[pl.BlockSpec(memory_space=pltpu.HBM)] * 8,
        out_specs=(vmem,) * 4,
        scratch_shapes=[
            pltpu.VMEM((768, COEF), f32),
            pltpu.VMEM((8, COEF, COEF), f32),
            pltpu.VMEM((CLASSES, COEF, COEF), f32),
            pltpu.VMEM((8, COEF, COEF), f32),
            pltpu.VMEM((48, 16), i32),
            pltpu.VMEM((96, COEF), f32),
            pltpu.VMEM((CLASSES, 2, CAPF), i32),
            pltpu.VMEM((CLASSES, 2, CAPP), i32),
            pltpu.VMEM((128, 128), f32),
            pltpu.VMEM((2, 768, 128), f32),
            pltpu.VMEM((TILES, COEF, 128), f32),
            pltpu.VMEM((TILES, 2 * COEF, 128), bf16),
            pltpu.VMEM((6, COEF, 128), f32),
            pltpu.VMEM((512, 256), f32),
            pltpu.VMEM((CLASSES, 160, 512), bf16),
            pltpu.VMEM((128, 384), f32),
            pltpu.VMEM((256, 128), f32),
            pltpu.VMEM((128, 128), f32),
            pltpu.VMEM((CLASSES, CAPF), i32),
            pltpu.VMEM((CLASSES, CAPP), i32),
            pltpu.VMEM((CLASSES, 2 * COEF, CAPF), bf16),
            pltpu.VMEM((CLASSES // 2, 2 * COEF, 256), bf16),
            pltpu.VMEM((CLASSES, 2 * COEF, CAPF), bf16),
            pltpu.VMEM((CLASSES // 2, 2 * COEF, 256), bf16),
            pltpu.VMEM((256, 128), f32),
            pltpu.SemaphoreType.DMA((8,)),
            pltpu.SemaphoreType.DMA((12,)),
            pltpu.SemaphoreType.DMA((12,)),
        ],
        compiler_params=pltpu.CompilerParams(
            collective_id=0, has_side_effects=True, vmem_limit_bytes=32 * 1024 * 1024
        ),
    )(
        *[pltpu.with_memory_space_constraint(v, pltpu.HBM) for v in (dens.reshape(768, COEF),
        occ.reshape(48, 16),
        coarse.reshape(96, COEF),
        up,
        maps,
        down,
        fp[0, 0],
        pp[0, 0])],
    )
    out = pl.pallas_call(
        finish,
        out_shape=jax.ShapeDtypeStruct((768, COEF), f32),
        in_specs=[vmem] * 4,
        out_specs=pl.BlockSpec(memory_space=pltpu.HBM),
        scratch_shapes=[
            pltpu.VMEM((2, 768, 128), f32),
            pltpu.VMEM((768, COEF), f32),
            pltpu.SemaphoreType.DMA((3,)),
        ],
        compiler_params=pltpu.CompilerParams(vmem_limit_bytes=8 * 1024 * 1024),
    )(*parts)
    return out.reshape(dens.shape)


def solution(mesh):
    shape = (mesh.shape["gx"], mesh.shape["gy"])
    return jax.shard_map(
        functools.partial(per_device, shape),
        mesh=mesh,
        in_specs=(
            P("gx", "gy", None, None),
            P("gx", "gy", None),
            P("gx", "gy", None, None),
            P(),
            P(),
            P(),
            P("gx", "gy", None, None, None),
            P("gx", "gy", None, None, None),
        ),
        out_specs=P("gx", "gy", None, None),
        check_vma=False,
    )
```

time: 43.7 us -> 34.2 us (0.78)
  the two profiles are of different devices: /device:TPU:221 before, /device:TPU:252 now
where the time goes in v2:
time: 34.2 us; the launch traced here: 34.1 us
  Pallas kernels  34.1 us (100%)
    pallas_call x1, Pallas kernels, per_device(): pl.pallas_call(functools.partial(kernel, shape), out_shape=(jax.ShapeDtyp...  32.7 us
    pallas_call x1, Pallas kernels, per_device(): pl.pallas_call(finish, out_shape=jax.ShapeDtypeStruct((768, COEF), f32),...  1.39 us

profile of v2, /device:TPU:252, one launch (start us, length us, event | category | flops | bytes accessed | tf_op | source)
XLA Modules:
  0.0 34.1 jit_solution(567026389030622947)
XLA Ops:
  0.0 32.7 %shard_map.82 = (f32[2,768,128]{2,1,0:T(8,128)S(1)}, bf16[2,96,152]{2,1,0:T(8,128)(2,1)S(1)}, bf16[8,2,152,152]{3,2,1,0:T(8,128)(2,1)S(1)}, f32[16,128]{1,0:T(8,128)S(1)}) custom-call(f32[768,152]{1,0:T(8,128)} %bitcast.6, s32[48,16]{1,0:T(8,128)} %bitcast.9, f32[96,152]{1,0:T(8,128)} %bitcast.7, f32[8,152,152]{2,1,0:T(8,128)} %up_hbm.1, ...), custom_call_target="tpu_custom_call" | custom-call | tf_op jit(solution)/shard_map/pallas_call | solution.py:409
  32.7 1.4 %shard_map.83 = f32[768,152]{1,0:T(8,128)} custom-call(f32[2,768,128]{2,1,0:T(8,128)S(1)} %get-tuple-element.9.sums, bf16[2,96,152]{2,1,0:T(8,128)(2,1)S(1)} %get-tuple-element.10.local, bf16[8,2,152,152]{3,2,1,0:T(8,128)(2,1)S(1)} %get-tuple-element.11.dmaps, f32[16,128]{1,0:T(8,128)S(1)} %get-tuple-element.12.mask), custom_call_target="tpu_custom_call" | custom-call | tf_op jit(solution)/shard_map/pallas_call | solution.py:462

commit v3 on v2

--- a/solution.py
+++ b/solution.py
@@ -74,7 +74,7 @@
     sums, local, dmaps, mask_out,
     dens, up, maps, down, occ, coarse, fp, pp,
     occ_pad, rows, frame, frame2, corner, tpad, tmaps,
-    tgt_pad, tgt_f, tgt_p, pos_f, pos_p, picked_f, picked_p, carried_f, carried_p, psum,
+    tgt_f, tgt_p, pos_f, pos_p, picked_f, picked_p, carried_f, carried_p, psum,
     load_sem, send_sem, recv_sem,
 ):
     mesh_x, mesh_y = shape
@@ -121,7 +121,6 @@
 
     occ_pad[...] = jnp.zeros_like(occ_pad)
     rows[1] = jnp.zeros((768, 128), f32)
-    tgt_pad[...] = jnp.zeros_like(tgt_pad)
     tpad[...] = jnp.zeros_like(tpad)
     psum[...] = jnp.zeros_like(psum)
 
@@ -213,7 +212,8 @@
         )[:, 0:COEF]
         chi, clo = split(child)
         uhi, ulo = split(up[k])
-        lifted = dot(chi, uhi) + (dot(clo, uhi) + dot(chi, ulo))
+        both = dot(jnp.concatenate([chi, clo], axis=0), uhi)
+        lifted = both[0:96, :] + (both[96:192, :] + dot(chi, ulo))
         parents = lifted if parents is None else parents + lifted
     parents = jnp.concatenate([parents, jnp.zeros((96, 256 - COEF), f32)], axis=1)
     for side, y0 in ((0, 0), (1, 2)):
@@ -236,10 +236,6 @@
     loads[4].wait()
     pos_f[...] = fine_position(fp[:, 1, :])
     pos_p[...] = parent_position(pp[:, 1, :])
-    tgt_pad[0:16, 0:256] = fp[:, 0, :].astype(f32)
-    tgt_pad[0:16, 256:384] = pp[:, 0, :].astype(f32)
-    tgt_f[...] = tgt_pad[:, 0:256].T
-    tgt_p[...] = tgt_pad[:, 256:384].T
 
     sub = lax.broadcasted_iota(i32, (256, 256), 0)
 
@@ -262,8 +258,20 @@
         g3 = jnp.concatenate([g, g[0:160, :], jnp.zeros((48, n), bf16)], axis=0)
         return stacked(dot(tmaps[c], g3)[0:COEF, :])
 
+    def turn_map(c, slot):
+        m = maps[c]
+        hi = m.astype(bf16).astype(f32)
+        tpad[slot, 0:152, 0:152] = hi
+        tpad[slot, 152:304, 0:152] = hi
+        tpad[slot, 304:456, 0:152] = m - hi
+        tmaps[c] = tpad[slot].T[0:160, :].astype(bf16)
+
+    loads[5].wait()
+
     def own_stage(h, carry):
-        for c in (2 * h, 2 * h + 1):
+        for n in range(2):
+            c = 2 * h + n
+            turn_map(c, n)
             picked_f[c] = pick(0, (0, 1, 2), pos_f[pl.ds(c, 1), :])
         return carry
 
@@ -274,19 +282,6 @@
     corner[4] = jnp.where(first, frame[6], pltpu.roll(frame[7], 64, 1))
     corner[5] = jnp.where(first, pltpu.roll(frame[6], 64, 1), frame[7])
     start(c_fine)
-
-    loads[5].wait()
-
-    def turn_map(c, carry):
-        m = maps[c]
-        hi = m.astype(bf16).astype(f32)
-        tpad[0:152, 0:152] = hi
-        tpad[152:304, 0:152] = hi
-        tpad[304:456, 0:152] = m - hi
-        tmaps[c] = tpad[...].T[0:160, :].astype(bf16)
-        return carry
-
-    lax.fori_loop(0, CLASSES, turn_map, 0)
 
     arrive(y_second)
     frame[17] = jnp.where(first, pltpu.roll(frame[12], 64, 1), frame[13])
@@ -304,6 +299,10 @@
         for c in (2 * h, 2 * h + 1):
             g = pick(0, (3, 4, 5), pos_f[pl.ds(c, 1), :])
             picked_f[c] = picked_f[c] + g
+            row = fp[pl.ds(c, 1), 0, :].astype(f32)
+            tgt_f[c] = jnp.broadcast_to(row, (128, CAPF)).T
+            row = pp[pl.ds(c, 1), 0, :].astype(f32)
+            tgt_p[c] = jnp.broadcast_to(row, (128, CAPP)).T
         return carry
 
     lax.fori_loop(0, CLASSES // 2, side_stage, 0)
@@ -314,18 +313,33 @@
 
     def last_stage(h, carry):
         for c in (2 * h, 2 * h + 1):
-            g = picked_f[c] + pick(0, (6, 7), pos_f[pl.ds(c, 1), :])
-            carried_f[c] = carry_over(c, g)
+            picked_f[c] = picked_f[c] + pick(0, (6, 7), pos_f[pl.ds(c, 1), :])
         picked_p[h] = pick(16, (0, 1), parent_place(h))
         return carry
 
     lax.fori_loop(0, CLASSES // 2, last_stage, 0)
 
-    fplane = lax.broadcasted_iota(i32, (256, 256), 1).astype(f32)
+    def transfer_stage(h, carry):
+        for n in range(4):
+            c = 4 * h + n
+            carried_f[c] = carry_over(c, picked_f[c])
+        return carry
+
+    lax.fori_loop(0, CLASSES // 4, transfer_stage, 0)
+
+    plane = lax.broadcasted_iota(i32, (256, 128), 1).astype(f32)
+    ones, zeros = jnp.ones((256, 128), f32), jnp.zeros((256, 128), f32)
     for n in range(3):
         total = None
         for c in range(CLASSES):
-            hot = jnp.where(fplane == tgt_f[:, c : c + 1] - n * 256.0, 1.0, 0.0).astype(bf16)
+            spread = tgt_f[c]
+            hot = jnp.concatenate(
+                [
+                    jnp.where(plane + (n * 256.0 + m) == spread, ones, zeros).astype(bf16)
+                    for m in (0.0, 128.0)
+                ],
+                axis=1,
+            )
             part = dot(carried_f[c], hot)
             total = part if total is None else total + part
         summed = total[0:COEF, :] + total[COEF : 2 * COEF, :]
@@ -337,21 +351,31 @@
     arrive(c_parent)
     doubled(20, 21)
 
-    def parent_stage(h, carry):
-        g = picked_p[h] + pick(16, (2,), parent_place(h))
-        carried_p[h] = jnp.concatenate(
-            [carry_over(2 * h, g[:, 0:128]), carry_over(2 * h + 1, g[:, 128:256])], axis=1
-        )
+    def parent_stage(q, carry):
+        for n in range(4):
+            h = 4 * q + n
+            picked_p[h] = picked_p[h] + pick(16, (2,), parent_place(h))
         return carry
 
-    lax.fori_loop(0, CLASSES // 2, parent_stage, 0, unroll=2)
+    lax.fori_loop(0, CLASSES // 8, parent_stage, 0)
+
+    def parent_transfer(q, carry):
+        for n in range(2):
+            h = 2 * q + n
+            g = picked_p[h]
+            carried_p[h] = jnp.concatenate(
+                [carry_over(2 * h, g[:, 0:128]), carry_over(2 * h + 1, g[:, 128:256])],
+                axis=1,
+            )
+        return carry
+
+    lax.fori_loop(0, CLASSES // 4, parent_transfer, 0)
 
     total = None
-    plane = lax.broadcasted_iota(i32, (128, 128), 1).astype(f32)
     for h in range(CLASSES // 2):
         hot = jnp.concatenate(
             [
-                jnp.where(plane == tgt_p[:, c : c + 1], 1.0, 0.0).astype(bf16)
+                jnp.where(plane[0:CAPP] == tgt_p[c], 1.0, 0.0).astype(bf16)
                 for c in (2 * h, 2 * h + 1)
             ],
             axis=0,
@@ -375,11 +399,13 @@
 
 def finish(sums, local, dmaps, mask, out_hbm, rows, out, sem):
     pad = jnp.zeros((96, 256 - COEF), f32)
-    lhi, llo = local[0], local[1]
+    lhi = local[0]
+    lboth = jnp.concatenate([local[0], local[1]], axis=0)
     rows[...] = sums[...]
     pushed = []
     for k in range(8):
-        p = dot(lhi, dmaps[k, 0]) + (dot(llo, dmaps[k, 0]) + dot(lhi, dmaps[k, 1]))
+        both = dot(lboth, dmaps[k, 0])
+        p = both[0:96, :] + (both[96:192, :] + dot(lhi, dmaps[k, 1]))
         pushed.append(jnp.concatenate([p, pad], axis=1))
     mask_t = mask[...]
     copies = []
@@ -430,11 +456,10 @@
             pltpu.VMEM((TILES, COEF, 128), f32),
             pltpu.VMEM((TILES, 2 * COEF, 128), bf16),
             pltpu.VMEM((6, COEF, 128), f32),
-            pltpu.VMEM((512, 256), f32),
+            pltpu.VMEM((2, 512, 256), f32),
             pltpu.VMEM((CLASSES, 160, 512), bf16),
-            pltpu.VMEM((128, 384), f32),
-            pltpu.VMEM((256, 128), f32),
-            pltpu.VMEM((128, 128), f32),
+            pltpu.VMEM((CLASSES, CAPF, 128), f32),
+            pltpu.VMEM((CLASSES, CAPP, 128), f32),
             pltpu.VMEM((CLASSES, CAPF), i32),
             pltpu.VMEM((CLASSES, CAPP), i32),
             pltpu.VMEM((CLASSES, 2 * COEF, CAPF), bf16),

time: 34.2 us -> 29.7 us (0.87)
  Pallas kernels: 34.1 us -> 29.7 us
    pallas_call x1, Pallas kernels: 32.7 us -> 28.3 us  [per_device(): pl.pallas_call(functools.partial(kernel, shape), out_shape=(jax.ShapeDtyp...]
where the time goes in v3:
time: 29.7 us
  Pallas kernels  29.7 us (100%)
    pallas_call x1, Pallas kernels, per_device(): pl.pallas_call(functools.partial(kernel, shape), out_shape=(jax.ShapeDtyp...  28.3 us
    pallas_call x1, Pallas kernels, per_device(): pl.pallas_call(finish, out_shape=jax.ShapeDtypeStruct((768, COEF), f32),...  1.39 us

profile of v3, /device:TPU:252, one launch (start us, length us, event | category | flops | bytes accessed | tf_op | source)
XLA Modules:
  0.0 29.7 jit_solution(3068045163891388968)
XLA Ops:
  0.0 28.3 %shard_map.82 = (f32[2,768,128]{2,1,0:T(8,128)S(1)}, bf16[2,96,152]{2,1,0:T(8,128)(2,1)S(1)}, bf16[8,2,152,152]{3,2,1,0:T(8,128)(2,1)S(1)}, f32[16,128]{1,0:T(8,128)S(1)}) custom-call(f32[768,152]{1,0:T(8,128)} %bitcast.6, s32[48,16]{1,0:T(8,128)} %bitcast.9, f32[96,152]{1,0:T(8,128)} %bitcast.7, f32[8,152,152]{2,1,0:T(8,128)} %up_hbm.1, ...), custom_call_target="tpu_custom_call" | custom-call | tf_op jit(solution)/shard_map/pallas_call | solution.py:435
  28.3 1.4 %shard_map.83 = f32[768,152]{1,0:T(8,128)} custom-call(f32[2,768,128]{2,1,0:T(8,128)S(1)} %get-tuple-element.9.sums, bf16[2,96,152]{2,1,0:T(8,128)(2,1)S(1)} %get-tuple-element.10.local, bf16[8,2,152,152]{3,2,1,0:T(8,128)(2,1)S(1)} %get-tuple-element.11.dmaps, f32[16,128]{1,0:T(8,128)S(1)} %get-tuple-element.12.mask), custom_call_target="tpu_custom_call" | custom-call | tf_op jit(solution)/shard_map/pallas_call | solution.py:487

commit v4 on v3

--- a/solution.py
+++ b/solution.py
@@ -283,10 +283,6 @@
     corner[5] = jnp.where(first, pltpu.roll(frame[6], 64, 1), frame[7])
     start(c_fine)
 
-    arrive(y_second)
-    frame[17] = jnp.where(first, pltpu.roll(frame[12], 64, 1), frame[13])
-    start(c_parent)
-
     loads[6].wait()
     for k in range(8):
         dhi, dlo = split(down[k])
@@ -306,6 +302,10 @@
         return carry
 
     lax.fori_loop(0, CLASSES // 2, side_stage, 0)
+
+    arrive(y_second)
+    frame[17] = jnp.where(first, pltpu.roll(frame[12], 64, 1), frame[13])
+    start(c_parent)
 
     arrive(x_parent)
     arrive(c_fine)

time: 29.7 us -> 26.8 us (0.902)
  the two profiles are of different devices: /device:TPU:252 before, /device:TPU:30 now
where the time goes in v4:
time: 26.8 us; the launch traced here: 26.7 us
  Pallas kernels  26.7 us (100%)
    pallas_call x1, Pallas kernels, per_device(): pl.pallas_call(functools.partial(kernel, shape), out_shape=(jax.ShapeDtyp...  25.3 us
    pallas_call x1, Pallas kernels, per_device(): pl.pallas_call(finish, out_shape=jax.ShapeDtypeStruct((768, COEF), f32),...  1.39 us

profile of v4, /device:TPU:30, one launch (start us, length us, event | category | flops | bytes accessed | tf_op | source)
XLA Modules:
  0.0 26.7 jit_solution(3235179362350919668)
XLA Ops:
  0.0 25.3 %shard_map.82 = (f32[2,768,128]{2,1,0:T(8,128)S(1)}, bf16[2,96,152]{2,1,0:T(8,128)(2,1)S(1)}, bf16[8,2,152,152]{3,2,1,0:T(8,128)(2,1)S(1)}, f32[16,128]{1,0:T(8,128)S(1)}) custom-call(f32[768,152]{1,0:T(8,128)} %bitcast.6, s32[48,16]{1,0:T(8,128)} %bitcast.9, f32[96,152]{1,0:T(8,128)} %bitcast.7, f32[8,152,152]{2,1,0:T(8,128)} %up_hbm.1, ...), custom_call_target="tpu_custom_call" | custom-call | tf_op jit(solution)/shard_map/pallas_call | solution.py:435
  25.3 1.4 %shard_map.83 = f32[768,152]{1,0:T(8,128)} custom-call(f32[2,768,128]{2,1,0:T(8,128)S(1)} %get-tuple-element.9.sums, bf16[2,96,152]{2,1,0:T(8,128)(2,1)S(1)} %get-tuple-element.10.local, bf16[8,2,152,152]{3,2,1,0:T(8,128)(2,1)S(1)} %get-tuple-element.11.dmaps, f32[16,128]{1,0:T(8,128)S(1)} %get-tuple-element.12.mask), custom_call_target="tpu_custom_call" | custom-call | tf_op jit(solution)/shard_map/pallas_call | solution.py:487

commit v5 on v4

--- a/solution.py
+++ b/solution.py
@@ -253,29 +253,31 @@
             [pos_p[pl.ds(2 * h, 1), :], pos_p[pl.ds(2 * h + 1, 1), :]], axis=1
         )
 
-    def carry_over(c, g):
-        n = g.shape[1]
-        g3 = jnp.concatenate([g, g[0:160, :], jnp.zeros((48, n), bf16)], axis=0)
-        return stacked(dot(tmaps[c], g3)[0:COEF, :])
-
-    def turn_map(c, slot):
-        m = maps[c]
+    def by_fours(stage):
+        lax.fori_loop(0, CLASSES // 4, lambda q, carry: (stage(q), carry)[1], 0)
+
+    def carry_over(q, n, g):
+        g3 = jnp.concatenate(
+            [g, g[0:160, :], jnp.zeros((48, g.shape[1]), bf16)], axis=0
+        )
+        return stacked(dot(tmaps[q, n], g3)[0:COEF, :])
+
+    def turn_map(q, n, slot):
+        m = maps[4 * q + n]
         hi = m.astype(bf16).astype(f32)
         tpad[slot, 0:152, 0:152] = hi
         tpad[slot, 152:304, 0:152] = hi
         tpad[slot, 304:456, 0:152] = m - hi
-        tmaps[c] = tpad[slot].T[0:160, :].astype(bf16)
+        tmaps[q, n] = tpad[slot].T[0:160, :].astype(bf16)
 
     loads[5].wait()
 
-    def own_stage(h, carry):
-        for n in range(2):
-            c = 2 * h + n
-            turn_map(c, n)
-            picked_f[c] = pick(0, (0, 1, 2), pos_f[pl.ds(c, 1), :])
-        return carry
-
-    lax.fori_loop(0, CLASSES // 2, own_stage, 0)
+    def own_stage(q):
+        for n in range(4):
+            turn_map(q, n, n % 2)
+            picked_f[q, n] = pick(0, (0, 1, 2), pos_f[pl.ds(4 * q + n, 1), :])
+
+    by_fours(own_stage)
 
     arrive(y_first)
     first = lax.broadcasted_iota(i32, (COEF, 128), 1) < 64
@@ -291,17 +293,15 @@
     arrive(x_fine)
     doubled(6, 7, 8, 9, 10, 11)
 
-    def side_stage(h, carry):
-        for c in (2 * h, 2 * h + 1):
+    def side_stage(q):
+        for n in range(4):
+            c = 4 * q + n
             g = pick(0, (3, 4, 5), pos_f[pl.ds(c, 1), :])
-            picked_f[c] = picked_f[c] + g
+            picked_f[q, n] = picked_f[q, n] + g
             row = fp[pl.ds(c, 1), 0, :].astype(f32)
-            tgt_f[c] = jnp.broadcast_to(row, (128, CAPF)).T
-            row = pp[pl.ds(c, 1), 0, :].astype(f32)
-            tgt_p[c] = jnp.broadcast_to(row, (128, CAPP)).T
-        return carry
-
-    lax.fori_loop(0, CLASSES // 2, side_stage, 0)
+            tgt_f[q, n] = jnp.broadcast_to(row, (128, CAPF)).T
+
+    by_fours(side_stage)
 
     arrive(y_second)
     frame[17] = jnp.where(first, pltpu.roll(frame[12], 64, 1), frame[13])
@@ -311,28 +311,29 @@
     arrive(c_fine)
     doubled(12, 13, 14, 15, 17, 18, 19)
 
-    def last_stage(h, carry):
-        for c in (2 * h, 2 * h + 1):
-            picked_f[c] = picked_f[c] + pick(0, (6, 7), pos_f[pl.ds(c, 1), :])
-        picked_p[h] = pick(16, (0, 1), parent_place(h))
-        return carry
-
-    lax.fori_loop(0, CLASSES // 2, last_stage, 0)
-
-    def transfer_stage(h, carry):
+    def last_stage(q):
         for n in range(4):
-            c = 4 * h + n
-            carried_f[c] = carry_over(c, picked_f[c])
-        return carry
-
-    lax.fori_loop(0, CLASSES // 4, transfer_stage, 0)
+            c = 4 * q + n
+            picked_f[q, n] = picked_f[q, n] + pick(0, (6, 7), pos_f[pl.ds(c, 1), :])
+            row = pp[pl.ds(c, 1), 0, :].astype(f32)
+            tgt_p[q, n] = jnp.broadcast_to(row, (128, CAPP)).T
+        for m in range(2):
+            picked_p[q, m] = pick(16, (0, 1), parent_place(2 * q + m))
+
+    by_fours(last_stage)
+
+    def transfer_stage(q):
+        for n in range(4):
+            carried_f[q, n] = carry_over(q, n, picked_f[q, n])
+
+    by_fours(transfer_stage)
 
     plane = lax.broadcasted_iota(i32, (256, 128), 1).astype(f32)
     ones, zeros = jnp.ones((256, 128), f32), jnp.zeros((256, 128), f32)
     for n in range(3):
         total = None
         for c in range(CLASSES):
-            spread = tgt_f[c]
+            spread = tgt_f[c // 4, c % 4]
             hot = jnp.concatenate(
                 [
                     jnp.where(plane + (n * 256.0 + m) == spread, ones, zeros).astype(bf16)
@@ -340,7 +341,7 @@
                 ],
                 axis=1,
             )
-            part = dot(carried_f[c], hot)
+            part = dot(carried_f[c // 4, c % 4], hot)
             total = part if total is None else total + part
         summed = total[0:COEF, :] + total[COEF : 2 * COEF, :]
         summed = jnp.concatenate([summed, jnp.zeros((104, 256), f32)], axis=0)
@@ -351,36 +352,33 @@
     arrive(c_parent)
     doubled(20, 21)
 
-    def parent_stage(q, carry):
-        for n in range(4):
-            h = 4 * q + n
-            picked_p[h] = picked_p[h] + pick(16, (2,), parent_place(h))
-        return carry
-
-    lax.fori_loop(0, CLASSES // 8, parent_stage, 0)
-
-    def parent_transfer(q, carry):
-        for n in range(2):
-            h = 2 * q + n
-            g = picked_p[h]
-            carried_p[h] = jnp.concatenate(
-                [carry_over(2 * h, g[:, 0:128]), carry_over(2 * h + 1, g[:, 128:256])],
+    def parent_stage(q):
+        for m in range(2):
+            g = pick(16, (2,), parent_place(2 * q + m))
+            picked_p[q, m] = picked_p[q, m] + g
+
+    by_fours(parent_stage)
+
+    def parent_transfer(q):
+        for m in range(2):
+            g = picked_p[q, m]
+            carried_p[q, m] = jnp.concatenate(
+                [carry_over(q, 2 * m, g[:, 0:128]), carry_over(q, 2 * m + 1, g[:, 128:256])],
                 axis=1,
             )
-        return carry
-
-    lax.fori_loop(0, CLASSES // 4, parent_transfer, 0)
+
+    by_fours(parent_transfer)
 
     total = None
     for h in range(CLASSES // 2):
         hot = jnp.concatenate(
             [
-                jnp.where(plane[0:CAPP] == tgt_p[c], 1.0, 0.0).astype(bf16)
+                jnp.where(plane[0:CAPP] == tgt_p[c // 4, c % 4], 1.0, 0.0).astype(bf16)
                 for c in (2 * h, 2 * h + 1)
             ],
             axis=0,
         )
-        part = dot(carried_p[h], hot)
+        part = dot(carried_p[h // 2, h % 2], hot)
         total = part if total is None else total + part
     psum[0:COEF, :] = total[0:COEF, :] + total[COEF : 2 * COEF, :]
     loads[7].wait()
@@ -457,15 +455,15 @@
             pltpu.VMEM((TILES, 2 * COEF, 128), bf16),
             pltpu.VMEM((6, COEF, 128), f32),
             pltpu.VMEM((2, 512, 256), f32),
-            pltpu.VMEM((CLASSES, 160, 512), bf16),
-            pltpu.VMEM((CLASSES, CAPF, 128), f32),
-            pltpu.VMEM((CLASSES, CAPP, 128), f32),
+            pltpu.VMEM((4, 4, 160, 512), bf16),
+            pltpu.VMEM((4, 4, CAPF, 128), f32),
+            pltpu.VMEM((4, 4, CAPP, 128), f32),
             pltpu.VMEM((CLASSES, CAPF), i32),
             pltpu.VMEM((CLASSES, CAPP), i32),
-            pltpu.VMEM((CLASSES, 2 * COEF, CAPF), bf16),
-            pltpu.VMEM((CLASSES // 2, 2 * COEF, 256), bf16),
-            pltpu.VMEM((CLASSES, 2 * COEF, CAPF), bf16),
-            pltpu.VMEM((CLASSES // 2, 2 * COEF, 256), bf16),
+            pltpu.VMEM((4, 4, 2 * COEF, CAPF), bf16),
+            pltpu.VMEM((4, 2, 2 * COEF, 256), bf16),
+            pltpu.VMEM((4, 4, 2 * COEF, CAPF), bf16),
+            pltpu.VMEM((4, 2, 2 * COEF, 256), bf16),
             pltpu.VMEM((256, 128), f32),
             pltpu.SemaphoreType.DMA((8,)),
             pltpu.SemaphoreType.DMA((12,)),

time: 26.8 us -> 25.7 us (0.959)
  Pallas kernels: 26.7 us -> 25.6 us
    pallas_call x1, Pallas kernels: 25.3 us -> 24.2 us  [per_device(): pl.pallas_call(functools.partial(kernel, shape), out_shape=(jax.ShapeDtyp...]
where the time goes in v5:
time: 25.7 us; the launch traced here: 25.6 us
  Pallas kernels  25.6 us (100%)
    pallas_call x1, Pallas kernels, per_device(): pl.pallas_call(functools.partial(kernel, shape), out_shape=(jax.ShapeDtyp...  24.2 us
    pallas_call x1, Pallas kernels, per_device(): pl.pallas_call(finish, out_shape=jax.ShapeDtypeStruct((768, COEF), f32),...  1.39 us

profile of v5, /device:TPU:30, one launch (start us, length us, event | category | flops | bytes accessed | tf_op | source)
XLA Modules:
  0.0 25.6 jit_solution(18267670800739046990)
XLA Ops:
  0.0 24.2 %shard_map.82 = (f32[2,768,128]{2,1,0:T(8,128)S(1)}, bf16[2,96,152]{2,1,0:T(8,128)(2,1)S(1)}, bf16[8,2,152,152]{3,2,1,0:T(8,128)(2,1)S(1)}, f32[16,128]{1,0:T(8,128)S(1)}) custom-call(f32[768,152]{1,0:T(8,128)} %bitcast.6, s32[48,16]{1,0:T(8,128)} %bitcast.9, f32[96,152]{1,0:T(8,128)} %bitcast.7, f32[8,152,152]{2,1,0:T(8,128)} %up_hbm.1, ...), custom_call_target="tpu_custom_call" | custom-call | tf_op jit(solution)/shard_map/pallas_call | solution.py:433
  24.2 1.4 %shard_map.83 = f32[768,152]{1,0:T(8,128)} custom-call(f32[2,768,128]{2,1,0:T(8,128)S(1)} %get-tuple-element.9.sums, bf16[2,96,152]{2,1,0:T(8,128)(2,1)S(1)} %get-tuple-element.10.local, bf16[8,2,152,152]{3,2,1,0:T(8,128)(2,1)S(1)} %get-tuple-element.11.dmaps, f32[16,128]{1,0:T(8,128)S(1)} %get-tuple-element.12.mask), custom_call_target="tpu_custom_call" | custom-call | tf_op jit(solution)/shard_map/pallas_call | solution.py:485

commit v6 on v5

--- a/solution.py
+++ b/solution.py
@@ -253,8 +253,10 @@
             [pos_p[pl.ds(2 * h, 1), :], pos_p[pl.ds(2 * h + 1, 1), :]], axis=1
         )
 
-    def by_fours(stage):
-        lax.fori_loop(0, CLASSES // 4, lambda q, carry: (stage(q), carry)[1], 0)
+    def by_fours(stage, unroll=1):
+        lax.fori_loop(
+            0, CLASSES // 4, lambda q, carry: (stage(q), carry)[1], 0, unroll=unroll
+        )
 
     def carry_over(q, n, g):
         g3 = jnp.concatenate(
@@ -357,7 +359,7 @@
             g = pick(16, (2,), parent_place(2 * q + m))
             picked_p[q, m] = picked_p[q, m] + g
 
-    by_fours(parent_stage)
+    by_fours(parent_stage, unroll=2)
 
     def parent_transfer(q):
         for m in range(2):
@@ -367,7 +369,7 @@
                 axis=1,
             )
 
-    by_fours(parent_transfer)
+    by_fours(parent_transfer, unroll=2)
 
     total = None
     for h in range(CLASSES // 2):

time: 25.7 us -> 25 us (0.973)
  Pallas kernels: 25.6 us -> 24.9 us
    pallas_call x1, Pallas kernels: 24.2 us -> 23.5 us  [per_device(): pl.pallas_call(functools.partial(kernel, shape), out_shape=(jax.ShapeDtyp...]
where the time goes in v6:
time: 25 us; the launch traced here: 24.9 us
  Pallas kernels  24.9 us (100%)
    pallas_call x1, Pallas kernels, per_device(): pl.pallas_call(functools.partial(kernel, shape), out_shape=(jax.ShapeDtyp...  23.5 us
    pallas_call x1, Pallas kernels, per_device(): pl.pallas_call(finish, out_shape=jax.ShapeDtypeStruct((768, COEF), f32),...  1.39 us

profile of v6, /device:TPU:30, one launch (start us, length us, event | category | flops | bytes accessed | tf_op | source)
XLA Modules:
  0.0 24.9 jit_solution(10001799109525400766)
XLA Ops:
  0.0 23.5 %shard_map.82 = (f32[2,768,128]{2,1,0:T(8,128)S(1)}, bf16[2,96,152]{2,1,0:T(8,128)(2,1)S(1)}, bf16[8,2,152,152]{3,2,1,0:T(8,128)(2,1)S(1)}, f32[16,128]{1,0:T(8,128)S(1)}) custom-call(f32[768,152]{1,0:T(8,128)} %bitcast.6, s32[48,16]{1,0:T(8,128)} %bitcast.9, f32[96,152]{1,0:T(8,128)} %bitcast.7, f32[8,152,152]{2,1,0:T(8,128)} %up_hbm.1, ...), custom_call_target="tpu_custom_call" | custom-call | tf_op jit(solution)/shard_map/pallas_call | solution.py:435
  23.6 1.4 %shard_map.83 = f32[768,152]{1,0:T(8,128)} custom-call(f32[2,768,128]{2,1,0:T(8,128)S(1)} %get-tuple-element.9.sums, bf16[2,96,152]{2,1,0:T(8,128)(2,1)S(1)} %get-tuple-element.10.local, bf16[8,2,152,152]{3,2,1,0:T(8,128)(2,1)S(1)} %get-tuple-element.11.dmaps, f32[16,128]{1,0:T(8,128)S(1)} %get-tuple-element.12.mask), custom_call_target="tpu_custom_call" | custom-call | tf_op jit(solution)/shard_map/pallas_call | solution.py:487
